TPU v7x, 256 devices: a whole 4x4x8 slice. The times are simulated.
256 devices in a mesh: seq: 16 (over y, x), row: 4 (over z_lo, core), col: 4 (over z_hi).
Axes of the slice: x: 4, y: 4, z: 8 (z_hi: 4, z_lo: 2; z = z_hi * 2 + z_lo), core: 2. Of those that a mesh axis runs over, the one named last changes fastest.
Arguments:
- activations: bfloat16 [16, 64, 8192], P(None, 'row', 'seq'), may hold values from -6 to 6
- gradients: bfloat16 [16, 64, 8192], P(None, 'col', 'seq'), may hold values from -6 to 6
- basis_in: bfloat16 [8192, 4096], P('seq', 'col'), may hold values from -0.0625 to 0.0625
- basis_out: bfloat16 [8192, 4096], P('seq', 'row'), may hold values from -0.0625 to 0.0625
- lengths: int32 [16], replicated, may hold values from 16 to 64
Outputs:
- corrections: float32 [4096, 4096], P(('row', 'seq'), 'col')
All inputs are finite; a program needn't handle non-finite values.
Results may differ from a plain program's by a relative error of at most 0.0023.
Values may be sent and summed in bfloat16 or wider, within the bound.
A program may use at most 64 MiB of HBM per device.

v0:
```python
import jax
import jax.numpy as jnp
from jax import lax
from jax.sharding import PartitionSpec as P


def in_blocks(shard, dim, length):
    before, after = (shard.shape[:dim], shard.shape[dim + 1 :])
    return jnp.moveaxis(shard.reshape(*before, length, -1, *after), dim, 0)


def sum_at_owner(shard, axis, dim):
    pieces = in_blocks(shard, dim, lax.axis_size(axis))
    arrived = lax.all_to_all(pieces, axis, split_axis=0, concat_axis=0, tiled=True)
    return arrived.sum(axis=0)


def from_everyone(shard, axis):
    length = lax.axis_size(axis)
    return lax.all_to_all(
        jnp.broadcast_to(shard[None], (length, *shard.shape)), axis, 0, 0, tiled=True
    )


def joined_along(pieces, dim):
    lengths = list(pieces.shape[1:])
    lengths[dim] *= pieces.shape[0]
    return jnp.moveaxis(pieces, 0, dim).reshape(lengths)


def gathered_copies(shard, axis, dim):
    pieces = from_everyone(shard, axis)
    return joined_along(pieces, dim)


def sum_at_owner_2(shard, axis, dim):
    length = lax.axis_size(axis)
    pieces = lax.all_to_all(in_blocks(shard, dim, length), axis, 0, 0, tiled=True)
    return jnp.sum(pieces.astype(jnp.float32), axis=0)


def turned_terms(tokens, basis):
    return jnp.einsum("ntf,fk->ntk", tokens, basis, preferred_element_type=jnp.float32)


def local(activations, gradients, basis_in, basis_out, lengths):
    seq_count = lax.axis_size("seq")
    seq_index = lax.axis_index("seq")
    length = lengths[seq_index]
    summed_in = sum_at_owner(turned_terms(activations, basis_in), "seq", 0)
    turned_in = summed_in[0].astype(jnp.bfloat16)
    summed_out = sum_at_owner(turned_terms(gradients, basis_out), "seq", 0)
    turned_out = summed_out[0].astype(jnp.bfloat16)
    every_in = gathered_copies(turned_in, "row", 0)
    every_out = gathered_copies(turned_out, "col", 0)
    slot_total = every_in.shape[0]
    slots = jnp.arange(slot_total)
    contract = (((0,), (0,)), ((), ()))
    kept = jnp.where((slots < length)[:, None], every_out, jnp.zeros((), jnp.bfloat16))
    product_tile = lax.dot_general(kept, every_in, contract, preferred_element_type=jnp.float32)
    squared = product_tile * product_tile / (seq_count * slot_total)
    return sum_at_owner_2(squared.astype(jnp.bfloat16), "seq", 0)


def solution(mesh):
    return jax.shard_map(
        local,
        mesh=mesh,
        in_specs=(
            P(None, "row", "seq"),
            P(None, "col", "seq"),
            P("seq", "col"),
            P("seq", "row"),
            P(),
        ),
        out_specs=P(("row", "seq"), "col"),
        check_vma=False,
    )
```

profile of v0, /device:TPU:2, one launch (start us, length us, event | category | flops | bytes accessed | tf_op | source)
XLA Modules:
  0.0 105.2 jit_solution(13111950368804016265)
XLA Ops:
  0.0 0.0 copy-start
  0.0 0.0 copy-start.1
  0.0 0.0 copy-start.2
  0.0 1.2 %copy-done = bf16[512,1024]{1,0:T(8,128)(2,1)S(1)} copy-done((bf16[512,1024]{1,0:T(8,128)(2,1)S(1)}, bf16[512,1024]{1,0:T(8,128)(2,1)}, u32[]{:S(2)}) %copy-start) | copy-done | bytes 1048600
  1.2 2.4 %convolution_bitcast_fusion = f32[16,1,16,1024]{3,2,1,0:T(8,128)} fusion(bf16[16,16,512]{2,1,0:T(8,128)(2,1)} %param.5, bf16[512,1024]{1,0:T(8,128)(2,1)S(1)} %copy-done), kind=kOutput, calls=%fused_computation.4 | convolution fusion | flops 268435456 | bytes 2359296 | tf_op jit(solution)/shard_map/ntf,fk->ntk/dot_general | solution.py:43
  3.6 7.5 %all-to-all-start.2 = ((f32[16,1,16,1024]{3,2,1,0:T(8,128)}), f32[16,1,16,1024]{3,2,1,0:T(8,128)S(1)}, u32[]{:S(2)}, u32[]{:S(2)}) async-start(f32[16,1,16,1024]{3,2,1,0:T(8,128)} %convolution_bitcast_fusion), calls=%async_computation.2 | async-start | bytes 2097152 | tf_op jit(solution)/shard_map/all_to_all | solution.py:14
  11.1 0.0 copy-done.1
  11.1 0.0 copy-done.2
  11.1 1.5 %convolution_bitcast_fusion.1 = f32[16,1,16,1024]{3,2,1,0:T(8,128)} fusion(bf16[16,16,512]{2,1,0:T(8,128)(2,1)S(1)} %copy-done.2, bf16[512,1024]{1,0:T(8,128)(2,1)S(1)} %copy-done.1), kind=kOutput, calls=%fused_computation.5 | convolution fusion | flops 268435456 | bytes 2359296 | tf_op jit(solution)/shard_map/ntf,fk->ntk/dot_general | solution.py:43
  12.5 0.0 copy-start.3
  12.5 14.3 %all-to-all-done.2 = f32[16,1,16,1024]{3,2,1,0:T(8,128)S(1)} async-done(((f32[16,1,16,1024]{3,2,1,0:T(8,128)}), f32[16,1,16,1024]{3,2,1,0:T(8,128)S(1)}, u32[]{:S(2)}, u32[]{:S(2)}) %all-to-all-start.2) | async-done | bytes 1048608 | tf_op jit(solution)/shard_map/all_to_all | solution.py:14
  26.9 5.4 %all-to-all-start = ((f32[16,1,16,1024]{3,2,1,0:T(8,128)}), f32[16,1,16,1024]{3,2,1,0:T(8,128)S(1)}, u32[]{:S(2)}, u32[]{:S(2)}) async-start(f32[16,1,16,1024]{3,2,1,0:T(8,128)} %convolution_bitcast_fusion.1), calls=%async_computation | async-start | bytes 2097152 | tf_op jit(solution)/shard_map/all_to_all | solution.py:14
  32.3 0.1 reduce_sum.28
  32.3 15.1 %all-to-all-done = f32[16,1,16,1024]{3,2,1,0:T(8,128)S(1)} async-done(((f32[16,1,16,1024]{3,2,1,0:T(8,128)}), f32[16,1,16,1024]{3,2,1,0:T(8,128)S(1)}, u32[]{:S(2)}, u32[]{:S(2)}) %all-to-all-start) | async-done | bytes 1048608 | tf_op jit(solution)/shard_map/all_to_all | solution.py:14
  47.4 0.7 broadcast_in_dim.28
  48.1 3.3 %all-to-all-start.3 = ((bf16[4,16,1024]{2,1,0:T(8,128)(2,1)}), bf16[4,16,1024]{2,1,0:T(8,128)(2,1)S(1)}, u32[]{:S(2)}, u32[]{:S(2)}) async-start(bf16[4,16,1024]{2,1,0:T(8,128)(2,1)} %broadcast_in_dim.28), calls=%async_computation.3 | async-start | bytes 262144 | tf_op jit(solution)/shard_map/all_to_all | solution.py:20
  51.4 0.1 reduce_sum.27
  51.5 4.5 %all-to-all-done.3 = bf16[4,16,1024]{2,1,0:T(8,128)(2,1)S(1)} async-done(((bf16[4,16,1024]{2,1,0:T(8,128)(2,1)}), bf16[4,16,1024]{2,1,0:T(8,128)(2,1)S(1)}, u32[]{:S(2)}, u32[]{:S(2)}) %all-to-all-start.3) | async-done | bytes 131104 | tf_op jit(solution)/shard_map/all_to_all | solution.py:20
  56.0 0.7 broadcast_in_dim.26
  56.6 8.5 %all-to-all-start.1 = ((bf16[4,16,1024]{2,1,0:T(8,128)(2,1)}), bf16[4,16,1024]{2,1,0:T(8,128)(2,1)S(1)}, u32[]{:S(2)}, u32[]{:S(2)}) async-start(bf16[4,16,1024]{2,1,0:T(8,128)(2,1)} %broadcast_in_dim.26), calls=%async_computation.1 | async-start | bytes 262144 | tf_op jit(solution)/shard_map/all_to_all | solution.py:20
  65.1 0.0 copy-done.3
  65.1 0.6 dynamic_slice.3
  65.7 0.6 add_compare_fusion
  66.3 7.5 %all-to-all-done.1 = bf16[4,16,1024]{2,1,0:T(8,128)(2,1)S(1)} async-done(((bf16[4,16,1024]{2,1,0:T(8,128)(2,1)}), bf16[4,16,1024]{2,1,0:T(8,128)(2,1)S(1)}, u32[]{:S(2)}, u32[]{:S(2)}) %all-to-all-start.1) | async-done | bytes 131104 | tf_op jit(solution)/shard_map/all_to_all | solution.py:20
  73.8 0.8 fusion.1
  74.7 29.4 %all_to_all.25 = bf16[16,64,1024]{2,1,0:T(8,128)(2,1)S(1)} all-to-all(bf16[16,64,1024]{2,1,0:T(8,128)(2,1)S(1)} %bitcast.25), channel_id=1, replica_groups=mesh['seq'=16,'row'=4,'col'=4] {'seq'}, dimensions={0} | all-to-all | bytes 4194304 | tf_op jit(solution)/shard_map/all_to_all | solution.py:38
  104.1 1.1 %convert_reduce_fusion = f32[64,1024]{1,0:T(8,128)} fusion(bf16[16,64,1024]{2,1,0:T(8,128)(2,1)S(1)} %all_to_all.25), kind=kLoop, calls=%fused_computation.3 | loop fusion | flops 2031616 | bytes 2359296 | tf_op jit(solution)/shard_map/reduce_sum | solution.py:39
Async XLA Ops:
  0.0 1.2 %copy-start = (bf16[512,1024]{1,0:T(8,128)(2,1)S(1)}, bf16[512,1024]{1,0:T(8,128)(2,1)}, u32[]{:S(2)}) copy-start(bf16[512,1024]{1,0:T(8,128)(2,1)} %param.7) | copy-start | bytes 3145732
  0.0 11.1 %copy-start.1 = (bf16[512,1024]{1,0:T(8,128)(2,1)S(1)}, bf16[512,1024]{1,0:T(8,128)(2,1)}, u32[]{:S(2)}) copy-start(bf16[512,1024]{1,0:T(8,128)(2,1)} %param.8) | copy-start | bytes 3145732
  0.0 11.1 %copy-start.2 = (bf16[16,16,512]{2,1,0:T(8,128)(2,1)S(1)}, bf16[16,16,512]{2,1,0:T(8,128)(2,1)}, u32[]{:S(2)}) copy-start(bf16[16,16,512]{2,1,0:T(8,128)(2,1)} %param.6) | copy-start | bytes 786436
  3.6 23.3 %all-to-all-start.2 = ((f32[16,1,16,1024]{3,2,1,0:T(8,128)}), f32[16,1,16,1024]{3,2,1,0:T(8,128)S(1)}, u32[]{:S(2)}, u32[]{:S(2)}) async-start(f32[16,1,16,1024]{3,2,1,0:T(8,128)} %convolution_bitcast_fusion), calls=%async_computation.2 | async-start | bytes 2097152 | tf_op jit(solution)/shard_map/all_to_all | solution.py:14
  12.5 52.6 %copy-start.3 = (s32[16]{0:T(128)S(1)}, s32[16]{0:T(128)}, u32[]{:S(2)}) copy-start(s32[16]{0:T(128)} %param.9) | copy-start | bytes 196
  26.9 20.6 %all-to-all-start = ((f32[16,1,16,1024]{3,2,1,0:T(8,128)}), f32[16,1,16,1024]{3,2,1,0:T(8,128)S(1)}, u32[]{:S(2)}, u32[]{:S(2)}) async-start(f32[16,1,16,1024]{3,2,1,0:T(8,128)} %convolution_bitcast_fusion.1), calls=%async_computation | async-start | bytes 2097152 | tf_op jit(solution)/shard_map/all_to_all | solution.py:14
  48.1 7.9 %all-to-all-start.3 = ((bf16[4,16,1024]{2,1,0:T(8,128)(2,1)}), bf16[4,16,1024]{2,1,0:T(8,128)(2,1)S(1)}, u32[]{:S(2)}, u32[]{:S(2)}) async-start(bf16[4,16,1024]{2,1,0:T(8,128)(2,1)} %broadcast_in_dim.28), calls=%async_computation.3 | async-start | bytes 262144 | tf_op jit(solution)/shard_map/all_to_all | solution.py:20
  56.6 17.2 %all-to-all-start.1 = ((bf16[4,16,1024]{2,1,0:T(8,128)(2,1)}), bf16[4,16,1024]{2,1,0:T(8,128)(2,1)S(1)}, u32[]{:S(2)}, u32[]{:S(2)}) async-start(bf16[4,16,1024]{2,1,0:T(8,128)(2,1)} %broadcast_in_dim.26), calls=%async_computation.1 | async-start | bytes 262144 | tf_op jit(solution)/shard_map/all_to_all | solution.py:20
where the time goes:
time: 106 us; the launch traced here: 105 us
  waiting for transfers between devices  41.4 us (39%)
  blocking collectives  29.4 us (28%)
  starting transfers between devices  24.7 us (23%)
  matrix products  4.62 us (4%)
  local copies, waits for them, and re-layouts  3.17 us (3%)
  other arithmetic  1.83 us (2%)
    all_to_all x1, blocking collectives, sum_at_owner_2(): lax.all_to_all(in_blocks(shard, dim, length), axis, 0, 0, tiled=True)  29.4 us
    all_to_all x2, waiting for transfers between devices, sum_at_owner(): lax.all_to_all(pieces, axis, split_axis=0, concat_axis=0, tiled=True)  29.4 us
    all_to_all x2, starting transfers between devices, sum_at_owner(): lax.all_to_all(pieces, axis, split_axis=0, concat_axis=0, tiled=True)  12.9 us
    all_to_all x2, waiting for transfers between devices, from_everyone(): lax.all_to_all(jnp.broadcast_to(shard[None], (length, *shard.shape)), axi...  12 us
    all_to_all x2, starting transfers between devices, from_everyone(): lax.all_to_all(jnp.broadcast_to(shard[None], (length, *shard.shape)), axi...  11.8 us
    dot_general x2, matrix products, turned_terms(): jnp.einsum('ntf,fk->ntk', tokens, basis, preferred_element_type=jnp.float32)  3.81 us
  transfers between devices with their start and end apart: 4, of which 4 were waited for; matrix products, arithmetic and copies ran while one was open for 3% of the time, Pallas kernels for 0%

commit v1 on v0

v1 whole, which is shorter than its diff:
```python
import functools

import jax
import jax.numpy as jnp
from jax import lax
from jax.experimental import pallas as pl
from jax.experimental.pallas import tpu as pltpu
from jax.sharding import PartitionSpec as P

MESH = pl.DeviceIdType.MESH
F32 = jnp.float32
BF16 = jnp.bfloat16

PHASES = dict(rs1_in=6, rs1_out=6, rs2_in=3, rs2_out=3, row=3, ag1=4, ag2=4, z=3, fwd=4, last=1)
FIRST = {}
TOTAL = 0
for _name, _count in PHASES.items():
    FIRST[_name] = TOTAL
    TOTAL += _count


def kernel(
    act_hbm, grad_hbm, bin_hbm, bout_hbm, len_ref, out_ref,
    act, grad, bin_, bout,
    p32_in, p16_in, p32_out, p16_out,
    got_in, got_out, tmp_in, tmp_out,
    q_in, q_out, got2_in, got2_out,
    t_in, gbuf, obuf, lhs, acc, xch,
    load_sem, send_sem, recv_sem,
):
    s = lax.axis_index("seq")
    r = lax.axis_index("row")
    c = lax.axis_index("col")
    y, x = lax.div(s, 4), lax.rem(s, 4)
    zl, k = lax.div(r, 2), lax.rem(r, 2)
    a = x + k * (y - x)
    b = y + k * (x - y)
    step_a, step_b = 1 + 3 * k, 4 - 3 * k

    def turn(v):
        return lax.rem(v + 4, 4)

    def at(a_, b_):
        return a_ * step_a + b_ * step_b

    def send(name, i, src, dst, device):
        n = FIRST[name] + i
        copy = pltpu.make_async_remote_copy(
            src_ref=src, dst_ref=dst, send_sem=send_sem.at[n], recv_sem=recv_sem.at[n],
            device_id=device, device_id_type=MESH,
        )
        copy.start()
        return copy

    loads = [
        pltpu.make_async_copy(src, dst, load_sem.at[i])
        for i, (src, dst) in enumerate(
            [(act_hbm, act), (bin_hbm, bin_), (grad_hbm, grad), (bout_hbm, bout)]
        )
    ]
    for load in loads:
        load.start()

    barrier = pltpu.get_barrier_semaphore()
    peers = []
    for d in (1, 2, 3):
        peers.append((at(turn(a + d), b), r, c))
        peers.append((at(a, turn(b + d)), r, c))
        peers.append((s, lax.rem(r + d, 4), c))
        peers.append((s, r, lax.rem(c + d, 4)))
    for peer in peers:
        pl.semaphore_signal(barrier, inc=1, device_id=peer, device_id_type=MESH)

    ap, am, a2 = turn(a + 1), turn(a - 1), turn(a + 2)
    bp, bm, b2 = turn(b + 1), turn(b - 1), turn(b + 2)
    right, left = (at(ap, b), r, c), (at(am, b), r, c)

    loads[0].wait()
    loads[1].wait()
    for j in range(4):
        m = jnp.dot(act[...], bin_[:, 256 * j : 256 * (j + 1)], preferred_element_type=F32)
        for i in range(4):
            blk = m[64 * i : 64 * (i + 1)]
            at_blk = i * step_a + j * step_b
            p32_in[at_blk] = blk
            p16_in[at_blk] = blk.astype(BF16)

    pl.semaphore_wait(barrier, len(peers))

    def ring1_start(name, p16, got):
        return [
            send(name, 0, p16.at[pl.ds(a2 * 4, 2)], got.at[0], right),
            send(name, 1, p16.at[pl.ds(a2 * 4 + 2, 2)], got.at[1], left),
            send(name, 2, p16.at[pl.ds(ap * 4 + 2, 2)], got.at[2], right),
            send(name, 3, p16.at[pl.ds(am * 4, 2)], got.at[3], left),
        ]

    def ring1_relay(name, copies, p32, got, tmp):
        copies[0].wait_recv()
        tmp[0] = (got[0].astype(F32) + p32[pl.ds(ap * 4, 2)]).astype(BF16)
        copies.append(send(name, 4, tmp.at[0], got.at[4], right))
        copies[1].wait_recv()
        tmp[1] = (got[1].astype(F32) + p32[pl.ds(am * 4 + 2, 2)]).astype(BF16)
        copies.append(send(name, 5, tmp.at[1], got.at[5], left))

    def ring1_end(copies, p32, got, q):
        copies[2].wait_recv()
        copies[3].wait_recv()
        copies[4].wait_recv()
        copies[5].wait_recv()
        q[0:2] = p32[pl.ds(a * 4, 2)] + got[3].astype(F32) + got[4].astype(F32)
        q[2:4] = p32[pl.ds(a * 4 + 2, 2)] + got[2].astype(F32) + got[5].astype(F32)

    def ring2_start(name, q, got2):
        return [
            send(name, d - 1, q.at[turn(b + d)], got2.at[d - 1], (at(a, turn(b + d)), r, c))
            for d in (2, 1, 3)
        ]

    def ring2_end(copies, q, got2):
        for copy in copies:
            copy.wait_recv()
        return q[b] + got2[0] + got2[1] + got2[2]

    pending = []
    rs1_in = ring1_start("rs1_in", p16_in, got_in)

    loads[2].wait()
    loads[3].wait()
    for j in range(4):
        m = jnp.dot(grad[...], bout[:, 256 * j : 256 * (j + 1)], preferred_element_type=F32)
        m = m.T
        for i in range(4):
            blk = m[64 * i : 64 * (i + 1)]
            at_blk = i * step_b + j * step_a
            p32_out[at_blk] = blk
            p16_out[at_blk] = blk.astype(BF16)
    rs1_out = ring1_start("rs1_out", p16_out, got_out)

    ring1_relay("rs1_in", rs1_in, p32_in, got_in, tmp_in)
    ring1_relay("rs1_out", rs1_out, p32_out, got_out, tmp_out)

    ring1_end(rs1_in, p32_in, got_in, q_in)
    rs2_in = ring2_start("rs2_in", q_in, got2_in)
    ring1_end(rs1_out, p32_out, got_out, q_out)
    rs2_out = ring2_start("rs2_out", q_out, got2_out)

    turned = ring2_end(rs2_in, q_in, got2_in).astype(BF16)
    t_in[0] = turned[:, :128]
    t_in[1] = turned[:, 128:]
    gbuf[a, b, r] = t_in[k]
    row = [
        send("row", 0, t_in.at[1 - k], gbuf.at[b, a, r], (s, 2 * zl + 1 - k, c)),
        send("row", 1, t_in.at[k], gbuf.at[a, b, r], (s, 2 * (1 - zl) + k, c)),
        send("row", 2, t_in.at[1 - k], gbuf.at[b, a, r], (s, 2 * (1 - zl) + 1 - k, c)),
    ]

    obuf[k, c] = ring2_end(rs2_out, q_out, got2_out).astype(BF16)
    partner = (s, 2 * zl + 1 - k, c)
    z = [
        send("z", d - 1, obuf.at[k, c], obuf.at[k, c], (s, r, turn(c + d)))
        for d in (2, 1, 3)
    ]
    fwd = [send("fwd", 0, obuf.at[k, c], obuf.at[k, c], partner)]

    for copy in row:
        copy.wait_recv()
    right_b, left_b = (at(a, bp), r, c), (at(a, bm), r, c)
    ag1 = [
        send("ag1", 0, gbuf.at[a, b], gbuf.at[a, b], right_b),
        send("ag1", 1, gbuf.at[a, b], gbuf.at[a, b], left_b),
    ]
    ag1[0].wait_recv()
    ag1.append(send("ag1", 2, gbuf.at[a, bm, pl.ds(0, 2)], gbuf.at[a, bm, pl.ds(0, 2)], right_b))
    ag1[1].wait_recv()
    ag1.append(send("ag1", 3, gbuf.at[a, bp, pl.ds(2, 2)], gbuf.at[a, bp, pl.ds(2, 2)], left_b))
    ag1[2].wait_recv()
    ag1[3].wait_recv()
    ag2 = [
        send("ag2", 0, gbuf.at[a], gbuf.at[a], right),
        send("ag2", 1, gbuf.at[a], gbuf.at[a], left),
    ]

    for i, d in enumerate((2, 1, 3)):
        z[i].wait_recv()
        from_ = turn(c - d)
        fwd.append(send("fwd", i + 1, obuf.at[k, from_], obuf.at[k, from_], partner))
    for copy in fwd:
        copy.wait_recv()

    lane = lax.broadcasted_iota(jnp.int32, (64, 256), 1)
    seq4 = lax.rem(lax.div(lane, 16), 4)
    slot = lax.div(lane, 64) * 16 + lax.rem(lane, 16)
    for g in range(4):
        keep = [
            jnp.logical_and(seq4 == i, slot < len_ref[4 * g + i]) for i in range(4)
        ]
        for kk in range(2):
            whole = jnp.concatenate(
                [obuf[kk, zz].astype(F32)[:, 64 * g : 64 * (g + 1)] for zz in range(4)], axis=1
            )
            for i in range(4):
                lhs[g, kk, i] = jnp.where(keep[i], whole, 0.0).astype(BF16)

    acc[...] = jnp.zeros_like(acc)

    def use(a_):
        for b_ in range(4):
            gy = b_ + k * (a_ - b_)
            gx = a_ + k * (b_ - a_)
            prod = jnp.dot(
                lhs[gy].reshape(512, 256), gbuf[a_, b_].reshape(256, 128),
                preferred_element_type=F32,
            )
            acc[:, gx] += jnp.sum((prod * prod).reshape(2, 4, 64, 128), axis=1)

    use(a)
    ag2[0].wait_recv()
    ag2.append(send("ag2", 2, gbuf.at[am, pl.ds(0, 2)], gbuf.at[am, pl.ds(0, 2)], right))
    ag2[1].wait_recv()
    ag2.append(send("ag2", 3, gbuf.at[ap, pl.ds(2, 2)], gbuf.at[ap, pl.ds(2, 2)], left))
    use(am)
    use(ap)
    ag2[2].wait_recv()
    ag2[3].wait_recv()
    use(a2)

    acc[...] = acc[...] * (1.0 / 1024.0)
    last = [send("last", 0, acc.at[1 - k], xch, partner)]
    for g in range(4):
        out_ref[:, pl.ds(pl.multiple_of(g * 256 + k * 128, 128), 128)] = acc[k, g]
    last[0].wait_recv()
    for g in range(4):
        out_ref[:, pl.ds(pl.multiple_of(g * 256 + (1 - k) * 128, 128), 128)] = xch[g]

    for copies in (rs1_in, rs1_out, rs2_in, rs2_out, row, z, fwd, ag1, ag2, last):
        for copy in copies:
            copy.wait_send()


def local(activations, gradients, basis_in, basis_out, lengths):
    any_ = pl.BlockSpec(memory_space=pl.ANY)
    vm = pltpu.VMEM
    return pl.pallas_call(
        kernel,
        out_shape=jax.ShapeDtypeStruct((64, 1024), F32),
        in_specs=[any_] * 4 + [pl.BlockSpec(memory_space=pltpu.SMEM)],
        out_specs=pl.BlockSpec(memory_space=pltpu.VMEM),
        scratch_shapes=[
            vm((256, 512), BF16), vm((256, 512), BF16),
            vm((512, 1024), BF16), vm((512, 1024), BF16),
            vm((16, 64, 256), F32), vm((16, 64, 256), BF16),
            vm((16, 64, 256), F32), vm((16, 64, 256), BF16),
            vm((6, 2, 64, 256), BF16), vm((6, 2, 64, 256), BF16),
            vm((2, 2, 64, 256), BF16), vm((2, 2, 64, 256), BF16),
            vm((4, 64, 256), F32), vm((4, 64, 256), F32),
            vm((3, 64, 256), F32), vm((3, 64, 256), F32),
            vm((2, 64, 128), BF16),
            vm((4, 4, 4, 64, 128), BF16),
            vm((2, 4, 64, 256), BF16),
            vm((4, 2, 4, 64, 256), BF16),
            vm((2, 4, 64, 128), F32),
            vm((4, 64, 128), F32),
            pltpu.SemaphoreType.DMA((4,)),
            pltpu.SemaphoreType.DMA((TOTAL,)),
            pltpu.SemaphoreType.DMA((TOTAL,)),
        ],
        compiler_params=pltpu.CompilerParams(
            collective_id=0, has_side_effects=True, vmem_limit_bytes=40 * 1024 * 1024
        ),
    )(
        activations.reshape(256, 512), gradients.reshape(256, 512),
        basis_in, basis_out, lengths,
    )


def solution(mesh):
    return jax.shard_map(
        local,
        mesh=mesh,
        in_specs=(
            P(None, "row", "seq"),
            P(None, "col", "seq"),
            P("seq", "col"),
            P("seq", "row"),
            P(),
        ),
        out_specs=P(("row", "seq"), "col"),
        check_vma=False,
    )
```

time: 106 us -> 51.1 us (0.48)
  the two profiles are of different devices: /device:TPU:2 before, /device:TPU:1 now
where the time goes in v1:
time: 51.1 us; the launch traced here: 50.3 us
  Pallas kernels  44.6 us (87%)
  local copies, waits for them, and re-layouts  5.71 us (11%)
    pallas_call x1, Pallas kernels, local(): pl.pallas_call(kernel, out_shape=jax.ShapeDtypeStruct((64, 1024), F32), i...  44.6 us
    unnamed x11, local copies, waits for them, and re-layouts  5.71 us

profile of v1, /device:TPU:1, one launch (start us, length us, event | category | flops | bytes accessed | tf_op | source)
XLA Modules:
  0.0 50.3 jit_solution(11061513860760324810)
XLA Ops:
  0.0 0.0 copy-start.4
  0.0 0.7 %copy-done.4 = s32[16]{0:T(128)S(1)} copy-done((s32[16]{0:T(128)S(1)}, s32[16]{0:T(128)}, u32[]{:S(2)}) %copy-start.4) | copy-done | bytes 88
  0.7 0.0 copy-start
  0.7 1.2 %copy-done = bf16[512,1024]{1,0:T(8,128)(2,1)S(1)} copy-done((bf16[512,1024]{1,0:T(8,128)(2,1)S(1)}, bf16[512,1024]{1,0:T(8,128)(2,1)}, u32[]{:S(2)}) %copy-start) | copy-done | bytes 1048600
  1.9 0.0 copy-start.1
  1.9 1.2 %copy-done.1 = bf16[512,1024]{1,0:T(8,128)(2,1)S(1)} copy-done((bf16[512,1024]{1,0:T(8,128)(2,1)S(1)}, bf16[512,1024]{1,0:T(8,128)(2,1)}, u32[]{:S(2)}) %copy-start.1) | copy-done | bytes 1048600
  3.1 0.0 copy-start.2
  3.1 0.9 %copy-done.2 = bf16[16,16,512]{2,1,0:T(8,128)(2,1)S(1)} copy-done((bf16[16,16,512]{2,1,0:T(8,128)(2,1)S(1)}, bf16[16,16,512]{2,1,0:T(8,128)(2,1)}, u32[]{:S(2)}) %copy-start.2) | copy-done | bytes 262168
  4.1 0.0 copy-start.3
  4.1 0.9 %copy-done.3 = bf16[16,16,512]{2,1,0:T(8,128)(2,1)S(1)} copy-done((bf16[16,16,512]{2,1,0:T(8,128)(2,1)S(1)}, bf16[16,16,512]{2,1,0:T(8,128)(2,1)}, u32[]{:S(2)}) %copy-start.3) | copy-done | bytes 262168
  5.0 44.6 %shard_map.55 = f32[64,1024]{1,0:T(8,128)S(1)} custom-call(bf16[256,512]{1,0:T(8,128)(2,1)S(1)} %bitcast.2, bf16[256,512]{1,0:T(8,128)(2,1)S(1)} %bitcast.3, bf16[512,1024]{1,0:T(8,128)(2,1)S(1)} %copy-done, bf16[512,1024]{1,0:T(8,128)(2,1)S(1)} %copy-done.1, s32[16]{0:T(128)S(1)} %copy-done.4), custom_call_target="tpu_custom_call" | custom-call | tf_op jit(solution)/shard_map/pallas_call | solution.py:244
  49.6 0.7 %copy.7 = f32[64,1024]{1,0:T(8,128)} copy(f32[64,1024]{1,0:T(8,128)S(1)} %shard_map.55) | data formatting | bytes 524288
Async XLA Ops:
  0.0 0.7 %copy-start.4 = (s32[16]{0:T(128)S(1)}, s32[16]{0:T(128)}, u32[]{:S(2)}) copy-start(s32[16]{0:T(128)} %len_ref.1) | copy-start | bytes 196
  0.7 1.2 %copy-start = (bf16[512,1024]{1,0:T(8,128)(2,1)S(1)}, bf16[512,1024]{1,0:T(8,128)(2,1)}, u32[]{:S(2)}) copy-start(bf16[512,1024]{1,0:T(8,128)(2,1)} %bin_hbm.1) | copy-start | bytes 3145732
  1.9 1.2 %copy-start.1 = (bf16[512,1024]{1,0:T(8,128)(2,1)S(1)}, bf16[512,1024]{1,0:T(8,128)(2,1)}, u32[]{:S(2)}) copy-start(bf16[512,1024]{1,0:T(8,128)(2,1)} %bout_hbm.1) | copy-start | bytes 3145732
  3.1 0.9 %copy-start.2 = (bf16[16,16,512]{2,1,0:T(8,128)(2,1)S(1)}, bf16[16,16,512]{2,1,0:T(8,128)(2,1)}, u32[]{:S(2)}) copy-start(bf16[16,16,512]{2,1,0:T(8,128)(2,1)} %param.5) | copy-start | bytes 786436
  4.1 0.9 %copy-start.3 = (bf16[16,16,512]{2,1,0:T(8,128)(2,1)S(1)}, bf16[16,16,512]{2,1,0:T(8,128)(2,1)}, u32[]{:S(2)}) copy-start(bf16[16,16,512]{2,1,0:T(8,128)(2,1)} %param.6) | copy-start | bytes 786436

commit v2 on v1

--- a/solution.py
+++ b/solution.py
@@ -266,7 +266,7 @@
             pltpu.SemaphoreType.DMA((TOTAL,)),
         ],
         compiler_params=pltpu.CompilerParams(
-            collective_id=0, has_side_effects=True, vmem_limit_bytes=40 * 1024 * 1024
+            collective_id=0, has_side_effects=True, vmem_limit_bytes=60 * 1024 * 1024
         ),
     )(
         activations.reshape(256, 512), gradients.reshape(256, 512),

time: 51.1 us -> 47.6 us (0.932)
  local copies, waits for them, and re-layouts: 5.71 us -> 1.67 us
  Pallas kernels: 44.6 us -> 45.3 us
    unnamed x11 -> x1, local copies, waits for them, and re-layouts: 5.71 us -> 1.67 us
    pallas_call x1, Pallas kernels: 44.6 us -> 45.3 us  [local(): pl.pallas_call(kernel, out_shape=jax.ShapeDtypeStruct((64, 1024), F32), i...]
where the time goes in v2:
time: 47.6 us; the launch traced here: 46.9 us
  Pallas kernels  45.3 us (95%)
  local copies, waits for them, and re-layouts  1.67 us (4%)
    pallas_call x1, Pallas kernels, local(): pl.pallas_call(kernel, out_shape=jax.ShapeDtypeStruct((64, 1024), F32), i...  45.3 us
    unnamed x1, local copies, waits for them, and re-layouts  1.67 us

profile of v2, /device:TPU:1, one launch (start us, length us, event | category | flops | bytes accessed | tf_op | source)
XLA Modules:
  0.0 46.9 jit_solution(9258572941583511693)
XLA Ops:
  0.0 45.3 %shard_map.55 = f32[64,1024]{1,0:T(8,128)} custom-call(bf16[256,512]{1,0:T(8,128)(2,1)} %bitcast.2, bf16[256,512]{1,0:T(8,128)(2,1)} %bitcast.3, bf16[512,1024]{1,0:T(8,128)(2,1)} %bin_hbm.1, bf16[512,1024]{1,0:T(8,128)(2,1)} %bout_hbm.1, s32[16]{0:T(128)} %len_ref.1), custom_call_target="tpu_custom_call" | custom-call | tf_op jit(solution)/shard_map/pallas_call | solution.py:244
  45.3 1.7 %copy.7 = f32[64,1024]{1,0:T(8,128)} copy(f32[64,1024]{1,0:T(8,128)} %shard_map.55) | data formatting | bytes 524288

commit v3 on v1

v3 whole, which is shorter than its diff:
```python
import jax
import jax.numpy as jnp
from jax import lax
from jax.experimental import pallas as pl
from jax.experimental.pallas import tpu as pltpu
from jax.sharding import PartitionSpec as P

MESH = pl.DeviceIdType.MESH
F32 = jnp.float32
BF16 = jnp.bfloat16

PHASES = dict(
    rs1_in=6, rs1_out=6, rs2_in=7, rs2_out=3, zx=1, ag1=6, ag2=32, z=3, fwd=4, last=4
)
FIRST = {}
TOTAL = 0
for _name, _count in PHASES.items():
    FIRST[_name] = TOTAL
    TOTAL += _count


def kernel(
    act_hbm, grad_hbm, bin_hbm, bout_hbm, len_ref, out_ref,
    act, grad, bin_, bout,
    p32_in, p16_in, p32_out, p16_out,
    got_in, got_out, tmp_in, tmp_out,
    q_in, q_out, same, cross, got2_out,
    gbuf, obuf, lhs, acc, xch,
    load_sem, send_sem, recv_sem,
):
    s = lax.axis_index("seq")
    r = lax.axis_index("row")
    c = lax.axis_index("col")
    y, x = lax.div(s, 4), lax.rem(s, 4)
    zl, k = lax.div(r, 2), lax.rem(r, 2)
    a = x + k * (y - x)
    b = y + k * (x - y)
    step_a, step_b = 1 + 3 * k, 4 - 3 * k

    def turn(v):
        return lax.rem(v + 4, 4)

    def at(a_, b_):
        return a_ * step_a + b_ * step_b

    started = []

    def send(name, i, src, dst, device):
        n = FIRST[name] + i
        copy = pltpu.make_async_remote_copy(
            src_ref=src, dst_ref=dst, send_sem=send_sem.at[n], recv_sem=recv_sem.at[n],
            device_id=device, device_id_type=MESH,
        )
        copy.start()
        started.append(copy)
        return copy

    loads = [
        pltpu.make_async_copy(src, dst, load_sem.at[i])
        for i, (src, dst) in enumerate(
            [(act_hbm, act), (bin_hbm, bin_), (grad_hbm, grad), (bout_hbm, bout)]
        )
    ]
    for load in loads:
        load.start()

    ap, am, a2 = turn(a + 1), turn(a - 1), turn(a + 2)
    other = 2 * zl + 1 - k
    partner = (s, other, c)
    right, left = (at(ap, b), r, c), (at(am, b), r, c)
    across = (s, 2 * (1 - zl) + k, c)

    barrier = pltpu.get_barrier_semaphore()
    peers = [right, left, partner, across]
    for d in (1, 2, 3):
        peers.append((at(a, turn(b + d)), r, c))
        peers.append((at(a, turn(b + d)), other, c))
        peers.append((at(turn(a + d), b), other, c))
        peers.append((s, r, turn(c + d)))
    for peer in peers:
        pl.semaphore_signal(barrier, inc=1, device_id=peer, device_id_type=MESH)

    loads[0].wait()
    loads[1].wait()
    for j in range(4):
        m = jnp.dot(act[...], bin_[:, 256 * j : 256 * (j + 1)], preferred_element_type=F32)
        for h in range(2):
            sc = h + k - 2 * h * k
            for i in range(4):
                blk = m[64 * i : 64 * (i + 1), 128 * h : 128 * (h + 1)]
                at_blk = 4 * j + i + 3 * (i - j) * sc
                p32_in[at_blk, sc] = blk
                p16_in[at_blk, sc] = blk.astype(BF16)

    pl.semaphore_wait(barrier, len(peers))

    def ring1_start(name, p16, got):
        return [
            send(name, 0, p16.at[pl.ds(a2 * 4, 2)], got.at[0], right),
            send(name, 1, p16.at[pl.ds(a2 * 4 + 2, 2)], got.at[1], left),
            send(name, 2, p16.at[pl.ds(ap * 4 + 2, 2)], got.at[2], right),
            send(name, 3, p16.at[pl.ds(am * 4, 2)], got.at[3], left),
        ]

    def ring1_relay(name, copies, p32, got, tmp):
        copies[0].wait_recv()
        tmp[0] = (got[0].astype(F32) + p32[pl.ds(ap * 4, 2)]).astype(BF16)
        copies.append(send(name, 4, tmp.at[0], got.at[4], right))
        copies[1].wait_recv()
        tmp[1] = (got[1].astype(F32) + p32[pl.ds(am * 4 + 2, 2)]).astype(BF16)
        copies.append(send(name, 5, tmp.at[1], got.at[5], left))

    def ring1_end(copies, p32, got, q):
        copies[2].wait_recv()
        copies[3].wait_recv()
        copies[4].wait_recv()
        q[0:2] = p32[pl.ds(a * 4, 2)] + got[3].astype(F32) + got[4].astype(F32)
        copies[5].wait_recv()
        q[2:4] = p32[pl.ds(a * 4 + 2, 2)] + got[2].astype(F32) + got[5].astype(F32)

    rs1_in = ring1_start("rs1_in", p16_in, got_in)

    loads[2].wait()
    loads[3].wait()
    for j in range(4):
        m = jnp.dot(grad[...], bout[:, 256 * j : 256 * (j + 1)], preferred_element_type=F32)
        m = m.T
        for i in range(4):
            blk = m[64 * i : 64 * (i + 1)]
            at_blk = 4 * i + j + 3 * (j - i) * k
            p32_out[at_blk] = blk
            p16_out[at_blk] = blk.astype(BF16)
    rs1_out = ring1_start("rs1_out", p16_out, got_out)

    ring1_relay("rs1_in", rs1_in, p32_in, got_in, tmp_in)
    ring1_relay("rs1_out", rs1_out, p32_out, got_out, tmp_out)

    ring1_end(rs1_in, p32_in, got_in, q_in)
    rs2_same, rs2_cross = [], []
    for d in (2, 1, 3):
        to = turn(b + d)
        rs2_same.append(
            send("rs2_in", d - 1, q_in.at[to, 0], same.at[d - 1], (at(a, to), r, c))
        )
        rs2_cross.append(
            send("rs2_in", 3 + d, q_in.at[to, 1], cross.at[d], (at(a, to), other, c))
        )
    rs2_cross.append(send("rs2_in", 3, q_in.at[b, 1], cross.at[0], partner))

    ring1_end(rs1_out, p32_out, got_out, q_out)
    rs2_out = [
        send("rs2_out", d - 1, q_out.at[turn(b + d)], got2_out.at[d - 1], (at(a, turn(b + d)), r, c))
        for d in (2, 1, 3)
    ]

    for copy in rs2_same + rs2_cross:
        copy.wait_recv()
    gbuf[a, b, zl, k] = (q_in[b, 0] + same[0] + same[1] + same[2]).astype(BF16)
    gbuf[a, b, zl, 1 - k] = (cross[0] + cross[1] + cross[2] + cross[3]).astype(BF16)

    def unit(a_, b_, w):
        return gbuf.at[a_, b_, w]

    def along_b(wi, w):
        return {
            d: send("ag1", 3 * wi + d - 1, unit(a, b, w), unit(a, b, w), (at(a, turn(b + d)), r, c))
            for d in (2, 1, 3)
        }

    def along_a(bi, wi, w):
        b_ = turn(b + bi)
        n = 4 * (4 * wi + bi)
        return [
            send("ag2", n, unit(a, b_, w), unit(a, b_, w), right),
            send("ag2", n + 1, unit(a, b_, w), unit(a, b_, w), left),
        ]

    def pass_on(copies, bi, wi, w):
        b_ = turn(b + bi)
        n = 4 * (4 * wi + bi)
        copies[0].wait_recv()
        copies.append(send("ag2", n + 2, gbuf.at[am, b_, w, 0], gbuf.at[am, b_, w, 0], right))
        copies[1].wait_recv()
        copies.append(send("ag2", n + 3, gbuf.at[ap, b_, w, 1], gbuf.at[ap, b_, w, 1], left))

    w0, w1 = zl, 1 - zl
    ring_a = {}
    zx = send("zx", 0, unit(a, b, w0), unit(a, b, w0), across)
    ring_b0 = along_b(0, w0)
    ring_a[0, 0] = along_a(0, 0, w0)

    for copy in rs2_out:
        copy.wait_recv()
    obuf[k, c] = (q_out[b] + got2_out[0] + got2_out[1] + got2_out[2]).astype(BF16)
    z = [
        send("z", d - 1, obuf.at[k, c], obuf.at[k, c], (s, r, turn(c + d)))
        for d in (2, 1, 3)
    ]
    fwd = [send("fwd", 0, obuf.at[k, c], obuf.at[k, c], partner)]

    zx.wait_recv()
    ring_b1 = along_b(1, w1)
    ring_a[0, 1] = along_a(0, 1, w1)
    for d in (1, 3):
        ring_b0[d].wait_recv()
        ring_a[4 - d, 0] = along_a(4 - d, 0, w0)
    pass_on(ring_a[0, 0], 0, 0, w0)
    ring_b0[2].wait_recv()
    ring_a[2, 0] = along_a(2, 0, w0)
    for d in (1, 3):
        ring_b1[d].wait_recv()
        ring_a[4 - d, 1] = along_a(4 - d, 1, w1)
    pass_on(ring_a[0, 1], 0, 1, w1)
    pass_on(ring_a[3, 0], 3, 0, w0)
    pass_on(ring_a[1, 0], 1, 0, w0)
    ring_b1[2].wait_recv()
    ring_a[2, 1] = along_a(2, 1, w1)

    for i, d in enumerate((2, 1, 3)):
        z[i].wait_recv()
        from_ = turn(c - d)
        fwd.append(send("fwd", i + 1, obuf.at[k, from_], obuf.at[k, from_], partner))
    pass_on(ring_a[2, 0], 2, 0, w0)
    pass_on(ring_a[3, 1], 3, 1, w1)
    pass_on(ring_a[1, 1], 1, 1, w1)
    for copy in fwd:
        copy.wait_recv()

    lane = lax.broadcasted_iota(jnp.int32, (64, 256), 1)
    seq4 = lax.rem(lax.div(lane, 16), 4)
    slot = lax.div(lane, 64) * 16 + lax.rem(lane, 16)
    for g in range(4):
        keep = [
            jnp.logical_and(seq4 == i, slot < len_ref[4 * g + i]) for i in range(4)
        ]
        for kk in range(2):
            whole = jnp.concatenate(
                [obuf[kk, zz].astype(F32)[:, 64 * g : 64 * (g + 1)] for zz in range(4)], axis=1
            )
            for i in range(4):
                lhs[g, kk, i] = jnp.where(keep[i], whole, 0.0).astype(BF16)
    pass_on(ring_a[2, 1], 2, 1, w1)

    last = []

    def use(i, a_):
        total = jnp.zeros((2, 64, 128), F32)
        for g in range(4):
            prod = jnp.dot(
                lhs[g].reshape(512, 256), gbuf[a_, g].reshape(256, 128),
                preferred_element_type=F32,
            )
            total += jnp.sum((prod * prod).reshape(2, 4, 64, 128), axis=1)
        acc[i] = total * (1.0 / 1024.0)
        last.append(send("last", i, acc.at[i, 1 - k], xch.at[i], partner))
        out_ref[:, pl.ds(pl.multiple_of(a_ * 256 + k * 128, 128), 128)] = acc[i, k]

    use(0, a)
    use(1, am)
    use(2, ap)
    for bi, wi in ((0, 0), (0, 1), (3, 0), (1, 0), (2, 0), (3, 1), (1, 1), (2, 1)):
        ring_a[bi, wi][2].wait_recv()
        ring_a[bi, wi][3].wait_recv()
    use(3, a2)

    for i, step in enumerate((0, 3, 1, 2)):
        last[i].wait_recv()
        at_col = turn(b + step) * 256 + (1 - k) * 128
        out_ref[:, pl.ds(pl.multiple_of(at_col, 128), 128)] = xch[i]

    for copy in started:
        copy.wait_send()


def local(activations, gradients, basis_in, basis_out, lengths):
    hbm = pl.BlockSpec(memory_space=pltpu.HBM)
    vm = pltpu.VMEM
    return pl.pallas_call(
        kernel,
        out_shape=jax.ShapeDtypeStruct((64, 1024), F32),
        in_specs=[hbm] * 4 + [pl.BlockSpec(memory_space=pltpu.SMEM)],
        out_specs=pl.BlockSpec(memory_space=pltpu.VMEM),
        scratch_shapes=[
            vm((256, 512), BF16), vm((256, 512), BF16),
            vm((512, 1024), BF16), vm((512, 1024), BF16),
            vm((16, 2, 64, 128), F32), vm((16, 2, 64, 128), BF16),
            vm((16, 64, 256), F32), vm((16, 64, 256), BF16),
            vm((6, 2, 2, 64, 128), BF16), vm((6, 2, 64, 256), BF16),
            vm((2, 2, 2, 64, 128), BF16), vm((2, 2, 64, 256), BF16),
            vm((4, 2, 64, 128), F32), vm((4, 64, 256), F32),
            vm((3, 64, 128), F32), vm((4, 64, 128), F32), vm((3, 64, 256), F32),
            vm((4, 4, 2, 2, 64, 128), BF16),
            vm((2, 4, 64, 256), BF16),
            vm((4, 2, 4, 64, 256), BF16),
            vm((4, 2, 64, 128), F32),
            vm((4, 64, 128), F32),
            pltpu.SemaphoreType.DMA((4,)),
            pltpu.SemaphoreType.DMA((TOTAL,)),
            pltpu.SemaphoreType.DMA((TOTAL,)),
        ],
        compiler_params=pltpu.CompilerParams(
            collective_id=0, has_side_effects=True, vmem_limit_bytes=40 * 1024 * 1024
        ),
    )(
        *[
            pltpu.with_memory_space_constraint(v, pltpu.HBM)
            for v in (
                activations.reshape(256, 512), gradients.reshape(256, 512), basis_in, basis_out
            )
        ],
        pltpu.with_memory_space_constraint(lengths, pltpu.HBM),
    )


def solution(mesh):
    return jax.shard_map(
        local,
        mesh=mesh,
        in_specs=(
            P(None, "row", "seq"),
            P(None, "col", "seq"),
            P("seq", "col"),
            P("seq", "row"),
            P(),
        ),
        out_specs=P(("row", "seq"), "col"),
        check_vma=False,
    )
```

time: 51.1 us -> 42 us (0.82); the launches traced: 50.3 us -> 41.9 us
  local copies, waits for them, and re-layouts: 5.71 us -> 0.71 us
  Pallas kernels: 44.6 us -> 41.2 us
    unnamed x11 -> x1, local copies, waits for them, and re-layouts: 5.71 us -> 0.71 us
    pallas_call x1, Pallas kernels: 44.6 us -> 41.2 us  [local(): pl.pallas_call(kernel, out_shape=jax.ShapeDtypeStruct((64, 1024), F32), i...]
where the time goes in v3:
time: 42 us; the launch traced here: 41.9 us
  Pallas kernels  41.2 us (98%)
  local copies, waits for them, and re-layouts  0.71 us (2%)
    pallas_call x1, Pallas kernels, local(): pl.pallas_call(kernel, out_shape=jax.ShapeDtypeStruct((64, 1024), F32), i...  41.2 us

profile of v3, /device:TPU:1, one launch (start us, length us, event | category | flops | bytes accessed | tf_op | source)
XLA Modules:
  0.0 41.9 jit_solution(12793534724830827765)
XLA Ops:
  0.0 41.2 %shard_map.55 = f32[64,1024]{1,0:T(8,128)S(1)} custom-call(bf16[256,512]{1,0:T(8,128)(2,1)} %bitcast.2, bf16[256,512]{1,0:T(8,128)(2,1)} %bitcast.3, bf16[512,1024]{1,0:T(8,128)(2,1)} %bin_hbm.1, bf16[512,1024]{1,0:T(8,128)(2,1)} %bout_hbm.1, s32[16]{0:T(128)} %len_ref.1), custom_call_target="tpu_custom_call" | custom-call | tf_op jit(solution)/shard_map/pallas_call | solution.py:278
  41.2 0.7 %copy.7 = f32[64,1024]{1,0:T(8,128)} copy(f32[64,1024]{1,0:T(8,128)S(1)} %shard_map.55) | data formatting | bytes 524288

commit v4 on v3

--- a/solution.py
+++ b/solution.py
@@ -10,7 +10,7 @@
 BF16 = jnp.bfloat16
 
 PHASES = dict(
-    rs1_in=6, rs1_out=6, rs2_in=7, rs2_out=3, zx=1, ag1=6, ag2=32, z=3, fwd=4, last=4
+    rs1_in=3, rs1_out=3, rs2_in=7, rs2_out=3, ag1=7, ag2=24, z=3, fwd=4, last=4
 )
 FIRST = {}
 TOTAL = 0
@@ -23,7 +23,7 @@
     act_hbm, grad_hbm, bin_hbm, bout_hbm, len_ref, out_ref,
     act, grad, bin_, bout,
     p32_in, p16_in, p32_out, p16_out,
-    got_in, got_out, tmp_in, tmp_out,
+    got_in, got_out,
     q_in, q_out, same, cross, got2_out,
     gbuf, obuf, lhs, acc, xch,
     load_sem, send_sem, recv_sem,
@@ -65,16 +65,19 @@
         load.start()
 
     ap, am, a2 = turn(a + 1), turn(a - 1), turn(a + 2)
+    bp, bm, b2 = turn(b + 1), turn(b - 1), turn(b + 2)
     other = 2 * zl + 1 - k
     partner = (s, other, c)
     right, left = (at(ap, b), r, c), (at(am, b), r, c)
-    across = (s, 2 * (1 - zl) + k, c)
+    over = 2 * (1 - zl) + k
+    far = (at(a2, b), r, c)
 
     barrier = pltpu.get_barrier_semaphore()
-    peers = [right, left, partner, across]
+    peers = [right, left, far, partner, (s, over, c)]
     for d in (1, 2, 3):
         peers.append((at(a, turn(b + d)), r, c))
         peers.append((at(a, turn(b + d)), other, c))
+        peers.append((at(a, turn(b + d)), over, c))
         peers.append((at(turn(a + d), b), other, c))
         peers.append((s, r, turn(c + d)))
     for peer in peers:
@@ -96,27 +99,17 @@
 
     def ring1_start(name, p16, got):
         return [
-            send(name, 0, p16.at[pl.ds(a2 * 4, 2)], got.at[0], right),
-            send(name, 1, p16.at[pl.ds(a2 * 4 + 2, 2)], got.at[1], left),
-            send(name, 2, p16.at[pl.ds(ap * 4 + 2, 2)], got.at[2], right),
-            send(name, 3, p16.at[pl.ds(am * 4, 2)], got.at[3], left),
+            send(name, d - 1, p16.at[pl.ds(turn(a + d) * 4, 4)], got.at[d - 1], to)
+            for d, to in ((2, far), (1, right), (3, left))
         ]
 
-    def ring1_relay(name, copies, p32, got, tmp):
-        copies[0].wait_recv()
-        tmp[0] = (got[0].astype(F32) + p32[pl.ds(ap * 4, 2)]).astype(BF16)
-        copies.append(send(name, 4, tmp.at[0], got.at[4], right))
-        copies[1].wait_recv()
-        tmp[1] = (got[1].astype(F32) + p32[pl.ds(am * 4 + 2, 2)]).astype(BF16)
-        copies.append(send(name, 5, tmp.at[1], got.at[5], left))
-
     def ring1_end(copies, p32, got, q):
-        copies[2].wait_recv()
-        copies[3].wait_recv()
-        copies[4].wait_recv()
-        q[0:2] = p32[pl.ds(a * 4, 2)] + got[3].astype(F32) + got[4].astype(F32)
-        copies[5].wait_recv()
-        q[2:4] = p32[pl.ds(a * 4 + 2, 2)] + got[2].astype(F32) + got[5].astype(F32)
+        for copy in copies:
+            copy.wait_recv()
+        q[...] = (
+            p32[pl.ds(a * 4, 4)]
+            + got[0].astype(F32) + got[1].astype(F32) + got[2].astype(F32)
+        )
 
     rs1_in = ring1_start("rs1_in", p16_in, got_in)
 
@@ -132,9 +125,6 @@
             p16_out[at_blk] = blk.astype(BF16)
     rs1_out = ring1_start("rs1_out", p16_out, got_out)
 
-    ring1_relay("rs1_in", rs1_in, p32_in, got_in, tmp_in)
-    ring1_relay("rs1_out", rs1_out, p32_out, got_out, tmp_out)
-
     ring1_end(rs1_in, p32_in, got_in, q_in)
     rs2_same, rs2_cross = [], []
     for d in (2, 1, 3):
@@ -161,33 +151,26 @@
     def unit(a_, b_, w):
         return gbuf.at[a_, b_, w]
 
-    def along_b(wi, w):
-        return {
-            d: send("ag1", 3 * wi + d - 1, unit(a, b, w), unit(a, b, w), (at(a, turn(b + d)), r, c))
-            for d in (2, 1, 3)
-        }
-
-    def along_a(bi, wi, w):
-        b_ = turn(b + bi)
-        n = 4 * (4 * wi + bi)
-        return [
-            send("ag2", n, unit(a, b_, w), unit(a, b_, w), right),
-            send("ag2", n + 1, unit(a, b_, w), unit(a, b_, w), left),
-        ]
-
-    def pass_on(copies, bi, wi, w):
-        b_ = turn(b + bi)
-        n = 4 * (4 * wi + bi)
-        copies[0].wait_recv()
-        copies.append(send("ag2", n + 2, gbuf.at[am, b_, w, 0], gbuf.at[am, b_, w, 0], right))
-        copies[1].wait_recv()
-        copies.append(send("ag2", n + 3, gbuf.at[ap, b_, w, 1], gbuf.at[ap, b_, w, 1], left))
+    def own_to(n, b_, row):
+        return send("ag1", n, unit(a, b, w0), unit(a, b, w0), (at(a, b_), row, c))
+
+    def along_a(bi, wi):
+        b_, w = turn(b + bi), (w0, w1)[wi]
+        for d, to in ((2, far), (1, right), (3, left)):
+            n = 3 * (4 * wi + bi) + d - 1
+            ring_a[bi, wi, d] = send("ag2", n, unit(a, b_, w), unit(a, b_, w), to)
 
     w0, w1 = zl, 1 - zl
     ring_a = {}
-    zx = send("zx", 0, unit(a, b, w0), unit(a, b, w0), across)
-    ring_b0 = along_b(0, w0)
-    ring_a[0, 0] = along_a(0, 0, w0)
+    along_a(0, 0)
+    near, away = {}, {}
+    near[2] = own_to(1, b2, r)
+    away[0] = own_to(3, b, over)
+    away[2] = own_to(5, b2, over)
+    near[1] = own_to(0, bp, r)
+    near[3] = own_to(2, bm, r)
+    away[1] = own_to(4, bp, over)
+    away[3] = own_to(6, bm, over)
 
     for copy in rs2_out:
         copy.wait_recv()
@@ -198,31 +181,23 @@
     ]
     fwd = [send("fwd", 0, obuf.at[k, c], obuf.at[k, c], partner)]
 
-    zx.wait_recv()
-    ring_b1 = along_b(1, w1)
-    ring_a[0, 1] = along_a(0, 1, w1)
+    away[0].wait_recv()
+    along_a(0, 1)
     for d in (1, 3):
-        ring_b0[d].wait_recv()
-        ring_a[4 - d, 0] = along_a(4 - d, 0, w0)
-    pass_on(ring_a[0, 0], 0, 0, w0)
-    ring_b0[2].wait_recv()
-    ring_a[2, 0] = along_a(2, 0, w0)
+        near[d].wait_recv()
+        along_a(4 - d, 0)
     for d in (1, 3):
-        ring_b1[d].wait_recv()
-        ring_a[4 - d, 1] = along_a(4 - d, 1, w1)
-    pass_on(ring_a[0, 1], 0, 1, w1)
-    pass_on(ring_a[3, 0], 3, 0, w0)
-    pass_on(ring_a[1, 0], 1, 0, w0)
-    ring_b1[2].wait_recv()
-    ring_a[2, 1] = along_a(2, 1, w1)
+        away[d].wait_recv()
+        along_a(4 - d, 1)
+    near[2].wait_recv()
+    along_a(2, 0)
+    away[2].wait_recv()
+    along_a(2, 1)
 
     for i, d in enumerate((2, 1, 3)):
         z[i].wait_recv()
         from_ = turn(c - d)
         fwd.append(send("fwd", i + 1, obuf.at[k, from_], obuf.at[k, from_], partner))
-    pass_on(ring_a[2, 0], 2, 0, w0)
-    pass_on(ring_a[3, 1], 3, 1, w1)
-    pass_on(ring_a[1, 1], 1, 1, w1)
     for copy in fwd:
         copy.wait_recv()
 
@@ -239,7 +214,6 @@
             )
             for i in range(4):
                 lhs[g, kk, i] = jnp.where(keep[i], whole, 0.0).astype(BF16)
-    pass_on(ring_a[2, 1], 2, 1, w1)
 
     last = []
 
@@ -256,12 +230,11 @@
         out_ref[:, pl.ds(pl.multiple_of(a_ * 256 + k * 128, 128), 128)] = acc[i, k]
 
     use(0, a)
-    use(1, am)
-    use(2, ap)
-    for bi, wi in ((0, 0), (0, 1), (3, 0), (1, 0), (2, 0), (3, 1), (1, 1), (2, 1)):
-        ring_a[bi, wi][2].wait_recv()
-        ring_a[bi, wi][3].wait_recv()
-    use(3, a2)
+    for i, d, a_ in ((1, 1, am), (2, 3, ap), (3, 2, a2)):
+        for wi in range(2):
+            for bi in range(4):
+                ring_a[bi, wi, d].wait_recv()
+        use(i, a_)
 
     for i, step in enumerate((0, 3, 1, 2)):
         last[i].wait_recv()
@@ -285,8 +258,7 @@
             vm((512, 1024), BF16), vm((512, 1024), BF16),
             vm((16, 2, 64, 128), F32), vm((16, 2, 64, 128), BF16),
             vm((16, 64, 256), F32), vm((16, 64, 256), BF16),
-            vm((6, 2, 2, 64, 128), BF16), vm((6, 2, 64, 256), BF16),
-            vm((2, 2, 2, 64, 128), BF16), vm((2, 2, 64, 256), BF16),
+            vm((3, 4, 2, 64, 128), BF16), vm((3, 4, 64, 256), BF16),
             vm((4, 2, 64, 128), F32), vm((4, 64, 256), F32),
             vm((3, 64, 128), F32), vm((4, 64, 128), F32), vm((3, 64, 256), F32),
             vm((4, 4, 2, 2, 64, 128), BF16),

time: 42 us -> 41.1 us (0.979)
  Pallas kernels: 41.2 us -> 40.3 us
    pallas_call x1, Pallas kernels: 41.2 us -> 40.3 us  [local(): pl.pallas_call(kernel, out_shape=jax.ShapeDtypeStruct((64, 1024), F32), i...]
where the time goes in v4:
time: 41.1 us; the launch traced here: 41 us
  Pallas kernels  40.3 us (98%)
  local copies, waits for them, and re-layouts  0.71 us (2%)
    pallas_call x1, Pallas kernels, local(): pl.pallas_call(kernel, out_shape=jax.ShapeDtypeStruct((64, 1024), F32), i...  40.3 us

profile of v4, /device:TPU:1, one launch (start us, length us, event | category | flops | bytes accessed | tf_op | source)
XLA Modules:
  0.0 41.0 jit_solution(64310667531210711)
XLA Ops:
  0.0 40.3 %shard_map.55 = f32[64,1024]{1,0:T(8,128)S(1)} custom-call(bf16[256,512]{1,0:T(8,128)(2,1)} %bitcast.2, bf16[256,512]{1,0:T(8,128)(2,1)} %bitcast.3, bf16[512,1024]{1,0:T(8,128)(2,1)} %bin_hbm.1, bf16[512,1024]{1,0:T(8,128)(2,1)} %bout_hbm.1, s32[16]{0:T(128)} %len_ref.1), custom_call_target="tpu_custom_call" | custom-call | tf_op jit(solution)/shard_map/pallas_call | solution.py:251
  40.3 0.7 %copy.7 = f32[64,1024]{1,0:T(8,128)} copy(f32[64,1024]{1,0:T(8,128)S(1)} %shard_map.55) | data formatting | bytes 524288

commit v5 on v4

--- a/solution.py
+++ b/solution.py
@@ -10,7 +10,7 @@
 BF16 = jnp.bfloat16
 
 PHASES = dict(
-    rs1_in=3, rs1_out=3, rs2_in=7, rs2_out=3, ag1=7, ag2=24, z=3, fwd=4, last=4
+    rs1_in=3, rs1_out=3, rs2_in=7, rs2_out=3, ag1=7, ag2=24, z=3, fw=13
 )
 FIRST = {}
 TOTAL = 0
@@ -24,9 +24,9 @@
     act, grad, bin_, bout,
     p32_in, p16_in, p32_out, p16_out,
     got_in, got_out,
-    q_in, q_out, same, cross, got2_out,
-    gbuf, obuf, lhs, acc, xch,
-    load_sem, send_sem, recv_sem,
+    q_in, q_out, q16_out, same, cross, got2_out,
+    gbuf, obuf, lhs, acc,
+    load_sem, send_sem, recv_sem, ready,
 ):
     s = lax.axis_index("seq")
     r = lax.axis_index("row")
@@ -55,14 +55,17 @@
         started.append(copy)
         return copy
 
-    loads = [
-        pltpu.make_async_copy(src, dst, load_sem.at[i])
-        for i, (src, dst) in enumerate(
-            [(act_hbm, act), (bin_hbm, bin_), (grad_hbm, grad), (bout_hbm, bout)]
-        )
+    def load(i, src, dst):
+        copy = pltpu.make_async_copy(src, dst, load_sem.at[i])
+        copy.start()
+        return copy
+
+    load_act = load(0, act_hbm, act)
+    load_bin = [
+        load(1 + j, bin_hbm.at[:, pl.ds(256 * j, 256)], bin_.at[:, pl.ds(256 * j, 256)])
+        for j in range(4)
     ]
-    for load in loads:
-        load.start()
+    load_out = [load(5, grad_hbm, grad), load(6, bout_hbm, bout)]
 
     ap, am, a2 = turn(a + 1), turn(a - 1), turn(a + 2)
     bp, bm, b2 = turn(b + 1), turn(b - 1), turn(b + 2)
@@ -73,19 +76,24 @@
     far = (at(a2, b), r, c)
 
     barrier = pltpu.get_barrier_semaphore()
-    peers = [right, left, far, partner, (s, over, c)]
+
+    def greet(s_, row_, c_):
+        pl.semaphore_signal(barrier, inc=1, device_id=(s_, row_, c_), device_id_type=MESH)
+
     for d in (1, 2, 3):
-        peers.append((at(a, turn(b + d)), r, c))
-        peers.append((at(a, turn(b + d)), other, c))
-        peers.append((at(a, turn(b + d)), over, c))
-        peers.append((at(turn(a + d), b), other, c))
-        peers.append((s, r, turn(c + d)))
-    for peer in peers:
-        pl.semaphore_signal(barrier, inc=1, device_id=peer, device_id_type=MESH)
-
-    loads[0].wait()
-    loads[1].wait()
+        for s_ in (at(turn(a + d), b), at(a, turn(b + d))):
+            greet(s_, 2 * zl, c)
+            greet(s_, 2 * (1 - zl), c)
+        greet(s, 2 * zl + 1, turn(c + d))
+    greet(s, 2 * (1 - zl), c)
+
+    @pl.when(k == 1)
+    def _():
+        greet(s, 2 * zl, c)
+
+    load_act.wait()
     for j in range(4):
+        load_bin[j].wait()
         m = jnp.dot(act[...], bin_[:, 256 * j : 256 * (j + 1)], preferred_element_type=F32)
         for h in range(2):
             sc = h + k - 2 * h * k
@@ -95,7 +103,14 @@
                 p32_in[at_blk, sc] = blk
                 p16_in[at_blk, sc] = blk.astype(BF16)
 
-    pl.semaphore_wait(barrier, len(peers))
+    @pl.when(k == 0)
+    def _():
+        pl.semaphore_wait(barrier, 27)
+        pl.semaphore_signal(ready, inc=1, device_id=partner, device_id_type=MESH)
+
+    @pl.when(k == 1)
+    def _():
+        pl.semaphore_wait(ready, 1)
 
     def ring1_start(name, p16, got):
         return [
@@ -113,8 +128,8 @@
 
     rs1_in = ring1_start("rs1_in", p16_in, got_in)
 
-    loads[2].wait()
-    loads[3].wait()
+    load_out[0].wait()
+    load_out[1].wait()
     for j in range(4):
         m = jnp.dot(grad[...], bout[:, 256 * j : 256 * (j + 1)], preferred_element_type=F32)
         m = m.T
@@ -138,18 +153,19 @@
     rs2_cross.append(send("rs2_in", 3, q_in.at[b, 1], cross.at[0], partner))
 
     ring1_end(rs1_out, p32_out, got_out, q_out)
+    q16_out[...] = q_out[...].astype(BF16)
     rs2_out = [
-        send("rs2_out", d - 1, q_out.at[turn(b + d)], got2_out.at[d - 1], (at(a, turn(b + d)), r, c))
+        send("rs2_out", d - 1, q16_out.at[turn(b + d)], got2_out.at[d - 1], (at(a, turn(b + d)), r, c))
         for d in (2, 1, 3)
     ]
 
     for copy in rs2_same + rs2_cross:
         copy.wait_recv()
-    gbuf[a, b, zl, k] = (q_in[b, 0] + same[0] + same[1] + same[2]).astype(BF16)
-    gbuf[a, b, zl, 1 - k] = (cross[0] + cross[1] + cross[2] + cross[3]).astype(BF16)
+    gbuf[k, a, b, zl, k] = (q_in[b, 0] + same[0] + same[1] + same[2]).astype(BF16)
+    gbuf[k, a, b, zl, 1 - k] = (cross[0] + cross[1] + cross[2] + cross[3]).astype(BF16)
 
     def unit(a_, b_, w):
-        return gbuf.at[a_, b_, w]
+        return gbuf.at[k, a_, b_, w]
 
     def own_to(n, b_, row):
         return send("ag1", n, unit(a, b, w0), unit(a, b, w0), (at(a, b_), row, c))
@@ -174,12 +190,23 @@
 
     for copy in rs2_out:
         copy.wait_recv()
-    obuf[k, c] = (q_out[b] + got2_out[0] + got2_out[1] + got2_out[2]).astype(BF16)
+    obuf[c] = (
+        q_out[b] + got2_out[0].astype(F32) + got2_out[1].astype(F32) + got2_out[2].astype(F32)
+    ).astype(BF16)
+
+    @pl.when(k == 1)
+    def _():
+        pl.semaphore_wait(barrier, 6)
+        pl.semaphore_signal(ready, inc=1, device_id=partner, device_id_type=MESH)
+
+    @pl.when(k == 0)
+    def _():
+        pl.semaphore_wait(ready, 1)
+
     z = [
-        send("z", d - 1, obuf.at[k, c], obuf.at[k, c], (s, r, turn(c + d)))
+        send("z", d - 1, obuf.at[c], obuf.at[c], (s, r, turn(c + d)))
         for d in (2, 1, 3)
     ]
-    fwd = [send("fwd", 0, obuf.at[k, c], obuf.at[k, c], partner)]
 
     away[0].wait_recv()
     along_a(0, 1)
@@ -194,52 +221,58 @@
     away[2].wait_recv()
     along_a(2, 1)
 
-    for i, d in enumerate((2, 1, 3)):
-        z[i].wait_recv()
-        from_ = turn(c - d)
-        fwd.append(send("fwd", i + 1, obuf.at[k, from_], obuf.at[k, from_], partner))
-    for copy in fwd:
+    order = (0, 3, 1, 2)
+    fw = {0: send("fw", 0, gbuf.at[k, a], gbuf.at[k, a], partner)}
+
+    def forward(bi):
+        b_ = turn(b + bi)
+        for i, (d, a_) in enumerate(((1, am), (3, ap), (2, a2))):
+            for wi in range(2):
+                ring_a[bi, wi, d].wait_recv()
+            n = 1 + 3 * bi + i
+            fw[n] = send("fw", n, gbuf.at[k, a_, b_], gbuf.at[k, a_, b_], partner)
+
+    for bi in order[:3]:
+        forward(bi)
+    for copy in z:
         copy.wait_recv()
 
     lane = lax.broadcasted_iota(jnp.int32, (64, 256), 1)
     seq4 = lax.rem(lax.div(lane, 16), 4)
     slot = lax.div(lane, 64) * 16 + lax.rem(lane, 16)
+    outs = [obuf[zz].astype(F32) for zz in range(4)]
     for g in range(4):
-        keep = [
-            jnp.logical_and(seq4 == i, slot < len_ref[4 * g + i]) for i in range(4)
-        ]
-        for kk in range(2):
-            whole = jnp.concatenate(
-                [obuf[kk, zz].astype(F32)[:, 64 * g : 64 * (g + 1)] for zz in range(4)], axis=1
+        whole = jnp.concatenate([v[:, 64 * g : 64 * (g + 1)] for v in outs], axis=1)
+        for i in range(4):
+            keep = jnp.logical_and(seq4 == i, slot < len_ref[4 * g + i])
+            lhs[g, i] = jnp.where(keep, whole, 0.0).astype(BF16)
+    forward(order[3])
+
+    acc[...] = jnp.zeros_like(acc)
+
+    def use(part, half, g):
+        left_side = lhs[g].reshape(256, 256)
+        for pair in range(2):
+            right_side = jnp.concatenate(
+                [gbuf[half, 2 * pair + i, g].reshape(256, 128) for i in range(2)], axis=1
             )
-            for i in range(4):
-                lhs[g, kk, i] = jnp.where(keep[i], whole, 0.0).astype(BF16)
-
-    last = []
-
-    def use(i, a_):
-        total = jnp.zeros((2, 64, 128), F32)
+            prod = jnp.dot(left_side, right_side, preferred_element_type=F32)
+            prod = prod * prod
+            acc[part, pair] += (prod[:64] + prod[64:128]) + (prod[128:192] + prod[192:])
+
+    fw[0].wait_recv()
+    for bi in order:
+        use(0, k, turn(b + bi))
+        for i in range(3):
+            fw[1 + 3 * bi + i].wait_recv()
+        use(1, 1 - k, turn(a + bi))
+
+    for part, half in ((0, k), (1, 1 - k)):
         for g in range(4):
-            prod = jnp.dot(
-                lhs[g].reshape(512, 256), gbuf[a_, g].reshape(256, 128),
-                preferred_element_type=F32,
-            )
-            total += jnp.sum((prod * prod).reshape(2, 4, 64, 128), axis=1)
-        acc[i] = total * (1.0 / 1024.0)
-        last.append(send("last", i, acc.at[i, 1 - k], xch.at[i], partner))
-        out_ref[:, pl.ds(pl.multiple_of(a_ * 256 + k * 128, 128), 128)] = acc[i, k]
-
-    use(0, a)
-    for i, d, a_ in ((1, 1, am), (2, 3, ap), (3, 2, a2)):
-        for wi in range(2):
-            for bi in range(4):
-                ring_a[bi, wi, d].wait_recv()
-        use(i, a_)
-
-    for i, step in enumerate((0, 3, 1, 2)):
-        last[i].wait_recv()
-        at_col = turn(b + step) * 256 + (1 - k) * 128
-        out_ref[:, pl.ds(pl.multiple_of(at_col, 128), 128)] = xch[i]
+            at_col = pl.multiple_of(g * 256 + half * 128, 128)
+            out_ref[:, pl.ds(at_col, 128)] = acc[
+                part, g // 2, :, 128 * (g % 2) : 128 * (g % 2 + 1)
+            ] * (1.0 / 1024.0)
 
     for copy in started:
         copy.wait_send()
@@ -259,16 +292,16 @@
             vm((16, 2, 64, 128), F32), vm((16, 2, 64, 128), BF16),
             vm((16, 64, 256), F32), vm((16, 64, 256), BF16),
             vm((3, 4, 2, 64, 128), BF16), vm((3, 4, 64, 256), BF16),
-            vm((4, 2, 64, 128), F32), vm((4, 64, 256), F32),
-            vm((3, 64, 128), F32), vm((4, 64, 128), F32), vm((3, 64, 256), F32),
-            vm((4, 4, 2, 2, 64, 128), BF16),
-            vm((2, 4, 64, 256), BF16),
-            vm((4, 2, 4, 64, 256), BF16),
-            vm((4, 2, 64, 128), F32),
-            vm((4, 64, 128), F32),
-            pltpu.SemaphoreType.DMA((4,)),
+            vm((4, 2, 64, 128), F32), vm((4, 64, 256), F32), vm((4, 64, 256), BF16),
+            vm((3, 64, 128), F32), vm((4, 64, 128), F32), vm((3, 64, 256), BF16),
+            vm((2, 4, 4, 2, 2, 64, 128), BF16),
+            vm((4, 64, 256), BF16),
+            vm((4, 4, 64, 256), BF16),
+            vm((2, 2, 64, 256), F32),
+            pltpu.SemaphoreType.DMA((7,)),
             pltpu.SemaphoreType.DMA((TOTAL,)),
             pltpu.SemaphoreType.DMA((TOTAL,)),
+            pltpu.SemaphoreType.REGULAR,
         ],
         compiler_params=pltpu.CompilerParams(
             collective_id=0, has_side_effects=True, vmem_limit_bytes=40 * 1024 * 1024

time: 41.1 us -> 34.1 us (0.83)
  Pallas kernels: 40.3 us -> 33.3 us
    pallas_call x1, Pallas kernels: 40.3 us -> 33.3 us  [local(): pl.pallas_call(kernel, out_shape=jax.ShapeDtypeStruct((64, 1024), F32), i...]
where the time goes in v5:
time: 34.1 us; the launch traced here: 34 us
  Pallas kernels  33.3 us (98%)
  local copies, waits for them, and re-layouts  0.71 us (2%)
    pallas_call x1, Pallas kernels, local(): pl.pallas_call(kernel, out_shape=jax.ShapeDtypeStruct((64, 1024), F32), i...  33.3 us
    unnamed x1, local copies, waits for them, and re-layouts  0.71 us

profile of v5, /device:TPU:1, one launch (start us, length us, event | category | flops | bytes accessed | tf_op | source)
XLA Modules:
  0.0 34.0 jit_solution(9872525925708609298)
XLA Ops:
  0.0 33.3 %shard_map.55 = f32[64,1024]{1,0:T(8,128)S(1)} custom-call(bf16[256,512]{1,0:T(8,128)(2,1)} %bitcast.2, bf16[256,512]{1,0:T(8,128)(2,1)} %bitcast.3, bf16[512,1024]{1,0:T(8,128)(2,1)} %bin_hbm.1, bf16[512,1024]{1,0:T(8,128)(2,1)} %bout_hbm.1, s32[16]{0:T(128)} %len_ref.1), custom_call_target="tpu_custom_call" | custom-call | tf_op jit(solution)/shard_map/pallas_call | solution.py:284
  33.3 0.7 %copy.7 = f32[64,1024]{1,0:T(8,128)} copy(f32[64,1024]{1,0:T(8,128)S(1)} %shard_map.55) | data formatting | bytes 524288

commit v6 on v5

--- a/solution.py
+++ b/solution.py
@@ -83,9 +83,9 @@
     for d in (1, 2, 3):
         for s_ in (at(turn(a + d), b), at(a, turn(b + d))):
             greet(s_, 2 * zl, c)
-            greet(s_, 2 * (1 - zl), c)
+            greet(s_, 2 * (1 - zl) + 1, c)
         greet(s, 2 * zl + 1, turn(c + d))
-    greet(s, 2 * (1 - zl), c)
+    greet(s, 2 * (1 - zl) + 1, c)
 
     @pl.when(k == 1)
     def _():
@@ -105,7 +105,7 @@
 
     @pl.when(k == 0)
     def _():
-        pl.semaphore_wait(barrier, 27)
+        pl.semaphore_wait(barrier, 13)
         pl.semaphore_signal(ready, inc=1, device_id=partner, device_id_type=MESH)
 
     @pl.when(k == 1)
@@ -176,6 +176,15 @@
             n = 3 * (4 * wi + bi) + d - 1
             ring_a[bi, wi, d] = send("ag2", n, unit(a, b_, w), unit(a, b_, w), to)
 
+    @pl.when(k == 1)
+    def _():
+        pl.semaphore_wait(barrier, 20)
+        pl.semaphore_signal(ready, inc=1, device_id=partner, device_id_type=MESH)
+
+    @pl.when(k == 0)
+    def _():
+        pl.semaphore_wait(ready, 1)
+
     w0, w1 = zl, 1 - zl
     ring_a = {}
     along_a(0, 0)
@@ -193,15 +202,6 @@
     obuf[c] = (
         q_out[b] + got2_out[0].astype(F32) + got2_out[1].astype(F32) + got2_out[2].astype(F32)
     ).astype(BF16)
-
-    @pl.when(k == 1)
-    def _():
-        pl.semaphore_wait(barrier, 6)
-        pl.semaphore_signal(ready, inc=1, device_id=partner, device_id_type=MESH)
-
-    @pl.when(k == 0)
-    def _():
-        pl.semaphore_wait(ready, 1)
 
     z = [
         send("z", d - 1, obuf.at[c], obuf.at[c], (s, r, turn(c + d)))

time: 34.1 us -> 34.2 us (level)
  no operation moved by 1% of the time
where the time goes in v6:
time: 34.2 us; the launch traced here: 34.1 us
  Pallas kernels  33.4 us (98%)
  local copies, waits for them, and re-layouts  0.71 us (2%)
    pallas_call x1, Pallas kernels, local(): pl.pallas_call(kernel, out_shape=jax.ShapeDtypeStruct((64, 1024), F32), i...  33.4 us
    unnamed x1, local copies, waits for them, and re-layouts  0.71 us

profile of v6, /device:TPU:1, one launch (start us, length us, event | category | flops | bytes accessed | tf_op | source)
XLA Modules:
  0.0 34.1 jit_solution(6551637247097834685)
XLA Ops:
  0.0 33.4 %shard_map.55 = f32[64,1024]{1,0:T(8,128)S(1)} custom-call(bf16[256,512]{1,0:T(8,128)(2,1)} %bitcast.2, bf16[256,512]{1,0:T(8,128)(2,1)} %bitcast.3, bf16[512,1024]{1,0:T(8,128)(2,1)} %bin_hbm.1, bf16[512,1024]{1,0:T(8,128)(2,1)} %bout_hbm.1, s32[16]{0:T(128)} %len_ref.1), custom_call_target="tpu_custom_call" | custom-call | tf_op jit(solution)/shard_map/pallas_call | solution.py:284
  33.4 0.7 %copy.7 = f32[64,1024]{1,0:T(8,128)} copy(f32[64,1024]{1,0:T(8,128)S(1)} %shard_map.55) | data formatting | bytes 524288
